TPU v7x, 32 devices: a whole 2x2x4 slice. The times are simulated.
32 devices in a mesh: comm: 4 (over z), arc: 8 (over y, x, core).
Axes of the slice: x: 2, y: 2, z: 4, core: 2. Of those that a mesh axis runs over, the one named last changes fastest.
Arguments:
- prev_dist: float32 [512, 2048], P('comm', 'arc'), may hold values from 0 to 4
- source_node: int32 [512], P('comm'), may hold values from 0 to 2047, as said below
- arc_tail: int32 [16, 2048], P(None, 'arc'), may hold values from 0 to 2047, as said below
- base_cost: float32 [16, 2048], P(None, 'arc'), may hold values from 0.05 to 1
- arc_price: float32 [16, 2048], P(None, 'arc'), may hold values from 0 to 1
- capacity: float32 [16, 2048], P(None, 'arc')
- path_arcs: int32 [512, 128], P(('comm', 'arc')), may hold values from 0 to 32767, as said below
- demand: float32 [512], P(('comm', 'arc')), may hold values from 0.5 to 2
Outputs:
- final_dist: float32 [512, 2048], P('comm', 'arc')
- new_price: float32 [16, 2048], P(None, 'arc')
Inputs may be any that keep to these rules, and one draw needn't show every extreme that they name: `arc_tail`: the tail of arc s * 2048 + v lies in a node block (nodes 128 b to 128 b + 127) at most 2 blocks before or after v's block, counted around the cycle of blocks. Row k is a walk: the head of path_arcs[k, h + 1] (its id modulo 2048) is the tail of path_arcs[k, h]. `source_node`: the tail of path_arcs[k, 127].
All inputs are finite; a program needn't handle non-finite values.
Results may differ from a plain program's by a relative error of at most 0.00002.
Values sent between devices are 32-bit elements; how exact they have to be, the bound alone decides.
No kernel may reach another device: no remote copies, remote signals or barrier semaphores. Data moves between devices by JAX's collectives and lax.ppermute only.
A program may use at most 64 MiB of HBM per device.

v0:
```python
import jax
import jax.numpy as jnp
from jax import lax
from jax.sharding import PartitionSpec as P

SWEEPS = 8
step_size = 0.25
eps_value = 1e-06


def with_halo(cells, sides, width):
    for axis, dim in sides:
        count = lax.axis_size(axis)
        head = lax.slice_in_dim(cells, 0, width, axis=dim)
        tail = lax.slice_in_dim(cells, cells.shape[dim] - width, cells.shape[dim], axis=dim)
        cells = jnp.concatenate(
            [
                lax.ppermute(tail, axis, [(i, (i + 1) % count) for i in range(count)]),
                cells,
                lax.ppermute(head, axis, [((i + 1) % count, i) for i in range(count)]),
            ],
            axis=dim,
        )
    return cells


def relax(window, window_start, tail_nodes, weights, current, node_count):
    degree = tail_nodes.shape[0]
    node_span = tail_nodes.shape[1]
    local_index = jnp.mod(tail_nodes - window_start, node_count).reshape(-1)
    picked = jnp.take(window, local_index, axis=0).reshape(degree, node_span, window.shape[1])
    candidate = picked + weights[:, :, None]
    return jnp.minimum(current, jnp.min(candidate, axis=0))


def shards(prev_dist, source_node, arc_tail, base_cost, arc_price, capacity, path_arcs, demand):
    shard_nodes = prev_dist.shape[1]
    arc_devices = lax.axis_size("arc")
    node_count = shard_nodes * arc_devices
    degree = arc_tail.shape[0]
    sweep_total = SWEEPS
    first_node = lax.axis_index("arc") * shard_nodes
    node_ids = first_node + jnp.arange(shard_nodes, dtype=jnp.int32)
    arc_weight = base_cost + arc_price
    node_major = jnp.where(node_ids[:, None] == source_node[None, :], jnp.float32(0.0), prev_dist.T)
    for sweep_number in range(sweep_total):
        window = with_halo(node_major, (("arc", 0),), shard_nodes)
        node_major = relax(
            window, first_node - shard_nodes, arc_tail, arc_weight, node_major, node_count
        )
    distance = node_major.T
    amounts = jnp.broadcast_to(demand[:, None], path_arcs.shape).reshape(-1)
    flattened = (
        jnp.zeros((degree * node_count,), jnp.float32).at[path_arcs.reshape(-1)].add(amounts)
    )
    partial_flow = lax.psum_scatter(
        flattened.reshape(degree, node_count), "arc", scatter_dimension=1, tiled=True
    )
    arc_flow = lax.psum(partial_flow, "comm")
    gradient = arc_flow - capacity
    square_sum = lax.psum(jnp.sum(gradient * gradient), "arc")
    scale_root = jnp.sqrt(square_sum / (degree * node_count) + eps_value)
    new_price = jnp.maximum(arc_price + step_size * gradient / scale_root, jnp.float32(0.0))
    return (distance, new_price)


def solution(mesh):
    in_specs = (
        P("comm", "arc"),
        P("comm"),
        P(None, "arc"),
        P(None, "arc"),
        P(None, "arc"),
        P(None, "arc"),
        P(("comm", "arc"), None),
        P(("comm", "arc")),
    )
    out_specs = (P("comm", "arc"), P(None, "arc"))
    return jax.shard_map(shards, mesh=mesh, in_specs=in_specs, out_specs=out_specs, check_vma=False)
```

profile of v0, /device:TPU:0, one launch (start us, length us, event | category | flops | bytes accessed | tf_op | source)
XLA Modules:
  0.0 245.0 jit_solution(11023003977533881316)
XLA Ops:
  7.2 1.0 copy.10
  8.2 0.8 bitcast_select_fusion
  9.0 3.4 %collective-permute-start.1 = (f32[256,128]{1,0:T(8,128)S(1)}, f32[256,128]{1,0:T(8,128)S(1)}, u32[]{:S(2)}, u32[]{:S(2)}) collective-permute-start(f32[256,128]{1,0:T(8,128)S(1)} %bitcast_select_fusion), channel_id=1, source_target_pairs={{1,0},{2,1},{3,2},{4,3},{5,4},{6,5},{7,6},{0,7},{9,8},{10,9},{11,1... | collective-permute-start | bytes 393224 | tf_op jit(solution)/shard_map/ppermute | solution.py:20
  12.4 0.7 compare_select_fusion
  13.2 11.3 %scatter_custom_fusion = f32[32768]{0:T(1024)S(1)} fusion(s32[2048]{0:T(1024)S(1)} %bitcast.60, f32[2048]{0:T(1024)S(1)} %broadcast_bitcast_fusion, f32[]{:T(128)} %constant.60.clone.1), kind=kCustom, calls=%fused_computation.42 | custom fusion | flops 2048 | bytes 131076 | tf_op jit(solution)/shard_map/scatter-add | solution.py:54
  25.2 0.7 fusion.3
  26.1 14.1 %gather_fusion = f32[4096,128]{1,0:T(8,128)} fusion(f32[768,128]{1,0:T(8,128)S(1)} %pad_maximum_fusion, s32[4096]{0:T(1024)S(1)} %fusion.4), kind=kCustom, calls=%fused_computation.clone | custom fusion | bytes 4210688 | tf_op jit(solution)/shard_map/jit(_take)/gather | solution.py:31
  40.2 20.2 %reduce-scatter.2.cloned.1.call-done = f32[16,256]{1,0:T(8,128)} async-done(((f32[16,2048]{1,0:T(8,128)}), f32[16,256]{1,0:T(8,128)}) %reduce-scatter.2.cloned.1.call-update) | async-done | bytes 16400 | tf_op jit(solution)/shard_map/reduce_scatter | solution.py:56
  60.4 19.4 %psum.14 = f32[16,256]{1,0:T(8,128)S(1)} all-reduce(f32[16,256]{1,0:T(8,128)} %reduce-scatter.2.cloned.1.call-done), channel_id=1, replica_groups=mesh['comm'=4,'arc'=8] {'comm'}, use_global_device_ids=true, to_apply=%region_10.12 | all-reduce | flops 4096 | bytes 32768 | tf_op jit(solution)/shard_map/psum | solution.py:59
  80.4 3.6 %broadcast_select_fusion.7 = f32[4096,128]{1,0:T(8,128)S(1)} fusion(f32[4096,128]{1,0:T(8,128)} %gather_fusion, pred[4096]{0:T(1024)(128)(4,1)S(1)} %compare_and_fusion), kind=kLoop, calls=%fused_computation.24 | loop fusion | flops 524288 | bytes 4198400 | tf_op jit(solution)/shard_map/jit(_take)/select_n | solution.py:31
  84.0 12.5 %psum.15 = f32[]{:T(128)} all-reduce(f32[]{:T(128)} %multiply_reduce_fusion), channel_id=1, replica_groups=mesh['comm'=4,'arc'=8] {'arc'}, use_global_device_ids=true, to_apply=%region_12.14 | all-reduce | flops 1 | bytes 8 | tf_op jit(solution)/shard_map/psum | solution.py:61
  99.2 2.5 %collective-permute-done.3 = f32[256,128]{1,0:T(8,128)S(1)} collective-permute-done((f32[256,128]{1,0:T(8,128)S(1)}, f32[256,128]{1,0:T(8,128)S(1)}, u32[]{:S(2)}, u32[]{:S(2)}) %collective-permute-start.3) | collective-permute-done | bytes 131104 | tf_op jit(solution)/shard_map/ppermute | solution.py:20
  101.7 3.7 %collective-permute-done.2 = f32[256,128]{1,0:T(8,128)S(1)} collective-permute-done((f32[256,128]{1,0:T(8,128)S(1)}, f32[256,128]{1,0:T(8,128)S(1)}, u32[]{:S(2)}, u32[]{:S(2)}) %collective-permute-start.2) | collective-permute-done | bytes 131104 | tf_op jit(solution)/shard_map/ppermute | solution.py:18
  105.4 10.8 %gather_fusion.1 = f32[4096,128]{1,0:T(8,128)S(1)} fusion(f32[768,128]{1,0:T(8,128)S(1)} %pad_maximum_fusion.1, s32[4096]{0:T(1024)S(1)} %fusion.4), kind=kCustom, calls=%fused_computation.1.clone | custom fusion | bytes 4210688 | tf_op jit(solution)/shard_map/jit(_take)/gather | solution.py:31
  116.2 2.1 broadcast_select_fusion.6
  118.4 0.7 add_reduce_fusion.6
  119.7 3.2 %collective-permute-done.5 = f32[256,128]{1,0:T(8,128)S(1)} collective-permute-done((f32[256,128]{1,0:T(8,128)S(1)}, f32[256,128]{1,0:T(8,128)S(1)}, u32[]{:S(2)}, u32[]{:S(2)}) %collective-permute-start.5) | collective-permute-done | bytes 131104 | tf_op jit(solution)/shard_map/ppermute | solution.py:20
  122.9 2.3 collective-permute-done.4
  125.2 10.8 %gather_fusion.2 = f32[4096,128]{1,0:T(8,128)S(1)} fusion(f32[768,128]{1,0:T(8,128)S(1)} %pad_maximum_fusion.2, s32[4096]{0:T(1024)S(1)} %fusion.4), kind=kCustom, calls=%fused_computation.2.clone | custom fusion | bytes 4210688 | tf_op jit(solution)/shard_map/jit(_take)/gather | solution.py:31
  136.0 2.1 broadcast_select_fusion.5
  138.2 0.7 add_reduce_fusion.5
  139.5 3.2 %collective-permute-done.7 = f32[256,128]{1,0:T(8,128)S(1)} collective-permute-done((f32[256,128]{1,0:T(8,128)S(1)}, f32[256,128]{1,0:T(8,128)S(1)}, u32[]{:S(2)}, u32[]{:S(2)}) %collective-permute-start.7) | collective-permute-done | bytes 131104 | tf_op jit(solution)/shard_map/ppermute | solution.py:20
  142.7 2.0 collective-permute-done.6
  144.7 10.8 %gather_fusion.3 = f32[4096,128]{1,0:T(8,128)S(1)} fusion(f32[768,128]{1,0:T(8,128)S(1)} %pad_maximum_fusion.3, s32[4096]{0:T(1024)S(1)} %fusion.4), kind=kCustom, calls=%fused_computation.3.clone | custom fusion | bytes 4210688 | tf_op jit(solution)/shard_map/jit(_take)/gather | solution.py:31
  155.5 2.1 broadcast_select_fusion.4
  157.7 0.7 add_reduce_fusion.4
  158.4 0.8 collective-permute-start.9
  159.2 2.9 %collective-permute-done.9 = f32[256,128]{1,0:T(8,128)S(1)} collective-permute-done((f32[256,128]{1,0:T(8,128)S(1)}, f32[256,128]{1,0:T(8,128)S(1)}, u32[]{:S(2)}, u32[]{:S(2)}) %collective-permute-start.9) | collective-permute-done | bytes 131104 | tf_op jit(solution)/shard_map/ppermute | solution.py:20
  162.2 2.3 collective-permute-done.8
  164.6 10.8 %gather_fusion.4 = f32[4096,128]{1,0:T(8,128)S(1)} fusion(f32[768,128]{1,0:T(8,128)S(1)} %pad_maximum_fusion.4, s32[4096]{0:T(1024)S(1)} %fusion.4), kind=kCustom, calls=%fused_computation.4.clone | custom fusion | bytes 4210688 | tf_op jit(solution)/shard_map/jit(_take)/gather | solution.py:31
  175.3 2.1 broadcast_select_fusion.3
  177.5 0.7 add_reduce_fusion.3
  178.8 3.2 %collective-permute-done.11 = f32[256,128]{1,0:T(8,128)S(1)} collective-permute-done((f32[256,128]{1,0:T(8,128)S(1)}, f32[256,128]{1,0:T(8,128)S(1)}, u32[]{:S(2)}, u32[]{:S(2)}) %collective-permute-start.11) | collective-permute-done | bytes 131104 | tf_op jit(solution)/shard_map/ppermute | solution.py:20
  182.0 2.0 collective-permute-done.10
  184.1 10.8 %gather_fusion.5 = f32[4096,128]{1,0:T(8,128)S(1)} fusion(f32[768,128]{1,0:T(8,128)S(1)} %pad_maximum_fusion.5, s32[4096]{0:T(1024)S(1)} %fusion.4), kind=kCustom, calls=%fused_computation.5.clone | custom fusion | bytes 4210688 | tf_op jit(solution)/shard_map/jit(_take)/gather | solution.py:31
  194.8 2.1 broadcast_select_fusion.2
  197.0 0.7 add_reduce_fusion.2
  197.7 0.8 collective-permute-start.13
  198.5 2.9 %collective-permute-done.13 = f32[256,128]{1,0:T(8,128)S(1)} collective-permute-done((f32[256,128]{1,0:T(8,128)S(1)}, f32[256,128]{1,0:T(8,128)S(1)}, u32[]{:S(2)}, u32[]{:S(2)}) %collective-permute-start.13) | collective-permute-done | bytes 131104 | tf_op jit(solution)/shard_map/ppermute | solution.py:20
  201.5 2.3 collective-permute-done.12
  203.9 10.8 %gather_fusion.6 = f32[4096,128]{1,0:T(8,128)S(1)} fusion(f32[768,128]{1,0:T(8,128)S(1)} %pad_maximum_fusion.6, s32[4096]{0:T(1024)S(1)} %fusion.4), kind=kCustom, calls=%fused_computation.6.clone | custom fusion | bytes 4210688 | tf_op jit(solution)/shard_map/jit(_take)/gather | solution.py:31
  214.6 2.1 broadcast_select_fusion.1
  216.8 0.7 add_reduce_fusion.1
  218.1 3.2 %collective-permute-done.15 = f32[256,128]{1,0:T(8,128)S(1)} collective-permute-done((f32[256,128]{1,0:T(8,128)S(1)}, f32[256,128]{1,0:T(8,128)S(1)}, u32[]{:S(2)}, u32[]{:S(2)}) %collective-permute-start.15) | collective-permute-done | bytes 131104 | tf_op jit(solution)/shard_map/ppermute | solution.py:20
  221.3 2.0 collective-permute-done.14
  223.4 10.8 %gather_fusion.7 = f32[4096,128]{1,0:T(8,128)S(1)} fusion(f32[768,128]{1,0:T(8,128)S(1)} %pad_maximum_fusion.7, s32[4096]{0:T(1024)S(1)} %fusion.4), kind=kCustom, calls=%fused_computation.7.clone | custom fusion | bytes 4210688 | tf_op jit(solution)/shard_map/jit(_take)/gather | solution.py:31
  234.1 2.1 broadcast_select_fusion
  237.4 0.8 copy.12
  (61 shorter events, 7.1 us)
Async XLA Ops:
  7.2 6.0 %copy-start = (f32[16]{0:T(128)S(1)}, f32[16]{0:T(128)}, u32[]{:S(2)}) copy-start(f32[16]{0:T(128)} %param.17) | copy-start | bytes 196
  7.2 53.2 %reduce-scatter.2.cloned.1.call-start = ((), (), s32[]{:S(2)}) async-start(), calls=%async_computation.1 | async-start | bytes 147456 | tf_op jit(solution)/shard_map/reduce_scatter | solution.py:56
  9.0 17.0 %collective-permute-start.1 = (f32[256,128]{1,0:T(8,128)S(1)}, f32[256,128]{1,0:T(8,128)S(1)}, u32[]{:S(2)}, u32[]{:S(2)}) collective-permute-start(f32[256,128]{1,0:T(8,128)S(1)} %bitcast_select_fusion), channel_id=1, source_target_pairs={{1,0},{2,1},{3,2},{4,3},{5,4},{6,5},{7,6},{0,7},{9,8},{10,9},{11,1... | collective-permute-start | bytes 393224 | tf_op jit(solution)/shard_map/ppermute | solution.py:20
  12.4 13.6 %collective-permute-start = (f32[256,128]{1,0:T(8,128)S(1)}, f32[256,128]{1,0:T(8,128)S(1)}, u32[]{:S(2)}, u32[]{:S(2)}) collective-permute-start(f32[256,128]{1,0:T(8,128)S(1)} %bitcast_select_fusion), channel_id=1, source_target_pairs={{0,1},{1,2},{2,3},{3,4},{4,5},{5,6},{6,7},{7,0},{8,9},{9,10},{10,1... | collective-permute-start | bytes 393224 | tf_op jit(solution)/shard_map/ppermute | solution.py:18
  26.1 53.7 %copy-start.5 = (f32[16,256]{1,0:T(8,128)S(1)}, f32[16,256]{1,0:T(8,128)}, u32[]{:S(2)}) copy-start(f32[16,256]{1,0:T(8,128)} %param.15) | copy-start | bytes 49156
  80.4 16.8 %copy-start.6 = (f32[16,256]{1,0:T(8,128)S(1)}, f32[16,256]{1,0:T(8,128)}, u32[]{:S(2)}) copy-start(f32[16,256]{1,0:T(8,128)} %param.14) | copy-start | bytes 49156
  80.4 16.8 %copy-start.7 = (f32[16,256]{1,0:T(8,128)S(1)}, f32[16,256]{1,0:T(8,128)}, u32[]{:S(2)}) copy-start(f32[16,256]{1,0:T(8,128)} %param.13) | copy-start | bytes 49156
  84.0 14.5 %copy-start.8 = (s32[128]{0:T(128)S(1)}, s32[128]{0:T(128)}, u32[]{:S(2)}) copy-start(s32[128]{0:T(128)} %param.11) | copy-start | bytes 1540
  98.5 17.7 %copy-start.3 = (f32[256,128]{1,0:T(8,128)}, f32[256,128]{1,0:T(8,128)S(1)}, u32[]{:S(2)}) copy-start(f32[256,128]{1,0:T(8,128)S(1)} %add_reduce_fusion.7) | copy-start | bytes 393220
  98.6 3.0 %collective-permute-start.3 = (f32[256,128]{1,0:T(8,128)S(1)}, f32[256,128]{1,0:T(8,128)S(1)}, u32[]{:S(2)}, u32[]{:S(2)}) collective-permute-start(f32[256,128]{1,0:T(8,128)S(1)} %fusion.5), channel_id=1, source_target_pairs={{1,0},{2,1},{3,2},{4,3},{5,4},{6,5},{7,6},{0,7},{9,8},{10,9},{11,1... | collective-permute-start | bytes 393224 | tf_op jit(solution)/shard_map/ppermute | solution.py:20
  98.7 6.7 %collective-permute-start.2 = (f32[256,128]{1,0:T(8,128)S(1)}, f32[256,128]{1,0:T(8,128)S(1)}, u32[]{:S(2)}, u32[]{:S(2)}) collective-permute-start(f32[256,128]{1,0:T(8,128)S(1)} %fusion.5), channel_id=1, source_target_pairs={{0,1},{1,2},{2,3},{3,4},{4,5},{5,6},{6,7},{7,0},{8,9},{9,10},{10,1... | collective-permute-start | bytes 393224 | tf_op jit(solution)/shard_map/ppermute | solution.py:18
  119.1 3.8 %collective-permute-start.5 = (f32[256,128]{1,0:T(8,128)S(1)}, f32[256,128]{1,0:T(8,128)S(1)}, u32[]{:S(2)}, u32[]{:S(2)}) collective-permute-start(f32[256,128]{1,0:T(8,128)S(1)} %min.49), channel_id=1, source_target_pairs={{1,0},{2,1},{3,2},{4,3},{5,4},{6,5},{7,6},{0,7},{9,8},{10,9},{11,1... | collective-permute-start | bytes 393224 | tf_op jit(solution)/shard_map/ppermute | solution.py:20
  119.2 6.0 %collective-permute-start.4 = (f32[256,128]{1,0:T(8,128)S(1)}, f32[256,128]{1,0:T(8,128)S(1)}, u32[]{:S(2)}, u32[]{:S(2)}) collective-permute-start(f32[256,128]{1,0:T(8,128)S(1)} %min.49), channel_id=1, source_target_pairs={{0,1},{1,2},{2,3},{3,4},{4,5},{5,6},{6,7},{7,0},{8,9},{9,10},{10,1... | collective-permute-start | bytes 393224 | tf_op jit(solution)/shard_map/ppermute | solution.py:18
  138.9 3.8 %collective-permute-start.7 = (f32[256,128]{1,0:T(8,128)S(1)}, f32[256,128]{1,0:T(8,128)S(1)}, u32[]{:S(2)}, u32[]{:S(2)}) collective-permute-start(f32[256,128]{1,0:T(8,128)S(1)} %min.51), channel_id=1, source_target_pairs={{1,0},{2,1},{3,2},{4,3},{5,4},{6,5},{7,6},{0,7},{9,8},{10,9},{11,1... | collective-permute-start | bytes 393224 | tf_op jit(solution)/shard_map/ppermute | solution.py:20
  139.4 5.3 %collective-permute-start.6 = (f32[256,128]{1,0:T(8,128)S(1)}, f32[256,128]{1,0:T(8,128)S(1)}, u32[]{:S(2)}, u32[]{:S(2)}) collective-permute-start(f32[256,128]{1,0:T(8,128)S(1)} %min.51), channel_id=1, source_target_pairs={{0,1},{1,2},{2,3},{3,4},{4,5},{5,6},{6,7},{7,0},{8,9},{9,10},{10,1... | collective-permute-start | bytes 393224 | tf_op jit(solution)/shard_map/ppermute | solution.py:18
  158.4 3.8 %collective-permute-start.9 = (f32[256,128]{1,0:T(8,128)S(1)}, f32[256,128]{1,0:T(8,128)S(1)}, u32[]{:S(2)}, u32[]{:S(2)}) collective-permute-start(f32[256,128]{1,0:T(8,128)S(1)} %min.53), channel_id=1, source_target_pairs={{1,0},{2,1},{3,2},{4,3},{5,4},{6,5},{7,6},{0,7},{9,8},{10,9},{11,1... | collective-permute-start | bytes 393224 | tf_op jit(solution)/shard_map/ppermute | solution.py:20
  159.2 5.3 %collective-permute-start.8 = (f32[256,128]{1,0:T(8,128)S(1)}, f32[256,128]{1,0:T(8,128)S(1)}, u32[]{:S(2)}, u32[]{:S(2)}) collective-permute-start(f32[256,128]{1,0:T(8,128)S(1)} %min.53), channel_id=1, source_target_pairs={{0,1},{1,2},{2,3},{3,4},{4,5},{5,6},{6,7},{7,0},{8,9},{9,10},{10,1... | collective-permute-start | bytes 393224 | tf_op jit(solution)/shard_map/ppermute | solution.py:18
  178.2 3.8 %collective-permute-start.11 = (f32[256,128]{1,0:T(8,128)S(1)}, f32[256,128]{1,0:T(8,128)S(1)}, u32[]{:S(2)}, u32[]{:S(2)}) collective-permute-start(f32[256,128]{1,0:T(8,128)S(1)} %min.55), channel_id=1, source_target_pairs={{1,0},{2,1},{3,2},{4,3},{5,4},{6,5},{7,6},{0,7},{9,8},{10,9},{11,1... | collective-permute-start | bytes 393224 | tf_op jit(solution)/shard_map/ppermute | solution.py:20
  178.7 5.3 %collective-permute-start.10 = (f32[256,128]{1,0:T(8,128)S(1)}, f32[256,128]{1,0:T(8,128)S(1)}, u32[]{:S(2)}, u32[]{:S(2)}) collective-permute-start(f32[256,128]{1,0:T(8,128)S(1)} %min.55), channel_id=1, source_target_pairs={{0,1},{1,2},{2,3},{3,4},{4,5},{5,6},{6,7},{7,0},{8,9},{9,10},{10,1... | collective-permute-start | bytes 393224 | tf_op jit(solution)/shard_map/ppermute | solution.py:18
  197.7 6.2 %copy-start.1 = (f32[256,128]{1,0:T(8,128)}, f32[256,128]{1,0:T(8,128)S(1)}, u32[]{:S(2)}) copy-start(f32[256,128]{1,0:T(8,128)S(1)} %add_reduce_fusion.2) | copy-start | bytes 393220
  197.7 3.8 %collective-permute-start.13 = (f32[256,128]{1,0:T(8,128)S(1)}, f32[256,128]{1,0:T(8,128)S(1)}, u32[]{:S(2)}, u32[]{:S(2)}) collective-permute-start(f32[256,128]{1,0:T(8,128)S(1)} %min.57), channel_id=1, source_target_pairs={{1,0},{2,1},{3,2},{4,3},{5,4},{6,5},{7,6},{0,7},{9,8},{10,9},{11,1... | collective-permute-start | bytes 393224 | tf_op jit(solution)/shard_map/ppermute | solution.py:20
  198.5 5.3 %collective-permute-start.12 = (f32[256,128]{1,0:T(8,128)S(1)}, f32[256,128]{1,0:T(8,128)S(1)}, u32[]{:S(2)}, u32[]{:S(2)}) collective-permute-start(f32[256,128]{1,0:T(8,128)S(1)} %min.57), channel_id=1, source_target_pairs={{0,1},{1,2},{2,3},{3,4},{4,5},{5,6},{6,7},{7,0},{8,9},{9,10},{10,1... | collective-permute-start | bytes 393224 | tf_op jit(solution)/shard_map/ppermute | solution.py:18
  217.5 3.8 %collective-permute-start.15 = (f32[256,128]{1,0:T(8,128)S(1)}, f32[256,128]{1,0:T(8,128)S(1)}, u32[]{:S(2)}, u32[]{:S(2)}) collective-permute-start(f32[256,128]{1,0:T(8,128)S(1)} %min.59), channel_id=1, source_target_pairs={{1,0},{2,1},{3,2},{4,3},{5,4},{6,5},{7,6},{0,7},{9,8},{10,9},{11,1... | collective-permute-start | bytes 393224 | tf_op jit(solution)/shard_map/ppermute | solution.py:20
  218.0 5.3 %collective-permute-start.14 = (f32[256,128]{1,0:T(8,128)S(1)}, f32[256,128]{1,0:T(8,128)S(1)}, u32[]{:S(2)}, u32[]{:S(2)}) collective-permute-start(f32[256,128]{1,0:T(8,128)S(1)} %min.59), channel_id=1, source_target_pairs={{0,1},{1,2},{2,3},{3,4},{4,5},{5,6},{6,7},{7,0},{8,9},{9,10},{10,1... | collective-permute-start | bytes 393224 | tf_op jit(solution)/shard_map/ppermute | solution.py:18
  236.3 0.9 copy-start.2
  236.3 1.0 copy-start.4
Sparse Core Ops, SparseCore 0:
  25.3 35.0 reduce-scatter.1
where the time goes:
time: 245 us
  local copies, waits for them, and re-layouts  92.3 us (38%)
  waiting for transfers between devices  58.3 us (24%)
  other arithmetic  39.5 us (16%)
  blocking collectives  31.8 us (13%)
  between operations  15.2 us (6%)
  starting transfers between devices  7.89 us (3%)
    gather x8, local copies, waits for them, and re-layouts, relax(): jnp.take(window, local_index, axis=0)  89.5 us
    ppermute x8, waiting for transfers between devices, with_halo(): lax.ppermute(head, axis, [((i + 1) % count, i) for i in range(count)])  21.2 us
    reduce_scatter x1, waiting for transfers between devices, shards(): lax.psum_scatter(flattened.reshape(degree, node_count), 'arc', scatter_di...  20.2 us
    psum x1, blocking collectives, shards(): arc_flow = lax.psum(partial_flow, 'comm')  19.4 us
    select_n x8, other arithmetic, relax(): jnp.take(window, local_index, axis=0)  18.6 us
    ppermute x8, waiting for transfers between devices, with_halo(): lax.ppermute(tail, axis, [(i, (i + 1) % count) for i in range(count)])  16.9 us
    psum x1, blocking collectives, shards(): square_sum = lax.psum(jnp.sum(gradient * gradient), 'arc')  12.5 us
    scatter-add x1, other arithmetic, shards(): jnp.zeros((degree * node_count,), jnp.float32).at[path_arcs.reshape(-1)]  11.3 us
  transfers between devices with their start and end apart: 17, of which 15 were waited for; matrix products, arithmetic and copies ran while one was open for 11% of the time, Pallas kernels for 0%

commit v1 on v0

--- a/solution.py
+++ b/solution.py
@@ -56,7 +56,7 @@
     partial_flow = lax.psum_scatter(
         flattened.reshape(degree, node_count), "arc", scatter_dimension=1, tiled=True
     )
-    arc_flow = lax.psum(partial_flow, "comm")
+    arc_flow = jnp.sum(lax.all_gather(partial_flow, "comm"), 0)
     gradient = arc_flow - capacity
     square_sum = lax.psum(jnp.sum(gradient * gradient), "arc")
     scale_root = jnp.sqrt(square_sum / (degree * node_count) + eps_value)

time: 245 us -> 239 us (0.976)
  blocking collectives: 31.8 us -> 25.9 us
    psum x1 -> x0, blocking collectives: 19.4 us -> none  [shards(): arc_flow = lax.psum(partial_flow, 'comm')]
    all_gather x0 -> x1, blocking collectives: none -> 13.5 us  [shards(): arc_flow = jnp.sum(lax.all_gather(partial_flow, 'comm'), 0)]
  transfers between devices with their start and end apart: 17 -> 17, of which waited for: 15 -> 15; matrix products, arithmetic and copies ran while one was open for 11% -> 12% of each run, Pallas kernels for 0% -> 0%
where the time goes in v1:
time: 239 us
  local copies, waits for them, and re-layouts  92.3 us (39%)
  waiting for transfers between devices  58.3 us (24%)
  other arithmetic  39.5 us (17%)
  blocking collectives  25.9 us (11%)
  between operations  15.2 us (6%)
  starting transfers between devices  7.89 us (3%)
    gather x8, local copies, waits for them, and re-layouts, relax(): jnp.take(window, local_index, axis=0)  89.5 us
    ppermute x8, waiting for transfers between devices, with_halo(): lax.ppermute(head, axis, [((i + 1) % count, i) for i in range(count)])  21.2 us
    reduce_scatter x1, waiting for transfers between devices, shards(): lax.psum_scatter(flattened.reshape(degree, node_count), 'arc', scatter_di...  20.2 us
    select_n x8, other arithmetic, relax(): jnp.take(window, local_index, axis=0)  18.6 us
    ppermute x8, waiting for transfers between devices, with_halo(): lax.ppermute(tail, axis, [(i, (i + 1) % count) for i in range(count)])  16.9 us
    all_gather x1, blocking collectives, shards(): arc_flow = jnp.sum(lax.all_gather(partial_flow, 'comm'), 0)  13.5 us
    psum x1, blocking collectives, shards(): square_sum = lax.psum(jnp.sum(gradient * gradient), 'arc')  12.5 us
    scatter-add x1, other arithmetic, shards(): jnp.zeros((degree * node_count,), jnp.float32).at[path_arcs.reshape(-1)]  11.3 us
  transfers between devices with their start and end apart: 17, of which 15 were waited for; matrix products, arithmetic and copies ran while one was open for 12% of the time, Pallas kernels for 0%

profile of v1, /device:TPU:0, one launch (start us, length us, event | category | flops | bytes accessed | tf_op | source)
XLA Modules:
  0.0 239.1 jit_solution(13242958989153119184)
XLA Ops:
  7.2 1.0 copy.13
  8.2 0.8 bitcast_select_fusion
  9.0 3.4 %collective-permute-start.1 = (f32[256,128]{1,0:T(8,128)S(1)}, f32[256,128]{1,0:T(8,128)S(1)}, u32[]{:S(2)}, u32[]{:S(2)}) collective-permute-start(f32[256,128]{1,0:T(8,128)S(1)} %bitcast_select_fusion), channel_id=1, source_target_pairs={{1,0},{2,1},{3,2},{4,3},{5,4},{6,5},{7,6},{0,7},{9,8},{10,9},{11,1... | collective-permute-start | bytes 393224 | tf_op jit(solution)/shard_map/ppermute | solution.py:20
  12.4 0.7 compare_select_fusion
  13.2 11.3 %scatter_custom_fusion = f32[32768]{0:T(1024)S(1)} fusion(s32[2048]{0:T(1024)S(1)} %bitcast.62, f32[2048]{0:T(1024)S(1)} %broadcast_bitcast_fusion, f32[]{:T(128)} %constant.60.clone.1), kind=kCustom, calls=%fused_computation.42 | custom fusion | flops 2048 | bytes 131076 | tf_op jit(solution)/shard_map/scatter-add | solution.py:54
  25.2 0.7 fusion.3
  26.1 14.1 %gather_fusion = f32[4096,128]{1,0:T(8,128)} fusion(f32[768,128]{1,0:T(8,128)S(1)} %pad_maximum_fusion, s32[4096]{0:T(1024)S(1)} %fusion.4), kind=kCustom, calls=%fused_computation.clone | custom fusion | bytes 4210688 | tf_op jit(solution)/shard_map/jit(_take)/gather | solution.py:31
  40.2 20.2 %reduce-scatter.2.cloned.1.call-done = f32[16,256]{1,0:T(8,128)} async-done(((f32[16,2048]{1,0:T(8,128)}), f32[16,256]{1,0:T(8,128)}) %reduce-scatter.2.cloned.1.call-update) | async-done | bytes 16400 | tf_op jit(solution)/shard_map/reduce_scatter | solution.py:56
  60.4 13.5 %all-gather = f32[64,256]{1,0:T(8,128)S(1)} all-gather(f32[16,256]{1,0:T(8,128)} %reduce-scatter.2.cloned.1.call-done), channel_id=2, replica_groups=mesh['comm'=4,'arc'=8] {'comm'}, dimensions={0}, use_global_device_ids=true | all-gather | bytes 81920 | tf_op jit(solution)/shard_map/all_gather | solution.py:59
  74.5 3.6 %broadcast_select_fusion.7 = f32[4096,128]{1,0:T(8,128)S(1)} fusion(f32[4096,128]{1,0:T(8,128)} %gather_fusion, pred[4096]{0:T(1024)(128)(4,1)S(1)} %compare_and_fusion), kind=kLoop, calls=%fused_computation.24 | loop fusion | flops 524288 | bytes 4198400 | tf_op jit(solution)/shard_map/jit(_take)/select_n | solution.py:31
  78.1 12.5 %psum.7 = f32[]{:T(128)} all-reduce(f32[]{:T(128)} %multiply_reduce_fusion), channel_id=1, replica_groups=mesh['comm'=4,'arc'=8] {'arc'}, use_global_device_ids=true, to_apply=%region_12.14 | all-reduce | flops 1 | bytes 8 | tf_op jit(solution)/shard_map/psum | solution.py:61
  93.3 2.5 %collective-permute-done.3 = f32[256,128]{1,0:T(8,128)S(1)} collective-permute-done((f32[256,128]{1,0:T(8,128)S(1)}, f32[256,128]{1,0:T(8,128)S(1)}, u32[]{:S(2)}, u32[]{:S(2)}) %collective-permute-start.3) | collective-permute-done | bytes 131104 | tf_op jit(solution)/shard_map/ppermute | solution.py:20
  95.8 3.7 %collective-permute-done.2 = f32[256,128]{1,0:T(8,128)S(1)} collective-permute-done((f32[256,128]{1,0:T(8,128)S(1)}, f32[256,128]{1,0:T(8,128)S(1)}, u32[]{:S(2)}, u32[]{:S(2)}) %collective-permute-start.2) | collective-permute-done | bytes 131104 | tf_op jit(solution)/shard_map/ppermute | solution.py:18
  99.6 10.8 %gather_fusion.1 = f32[4096,128]{1,0:T(8,128)S(1)} fusion(f32[768,128]{1,0:T(8,128)S(1)} %pad_maximum_fusion.1, s32[4096]{0:T(1024)S(1)} %fusion.4), kind=kCustom, calls=%fused_computation.1.clone | custom fusion | bytes 4210688 | tf_op jit(solution)/shard_map/jit(_take)/gather | solution.py:31
  110.3 2.1 broadcast_select_fusion.6
  112.5 0.7 add_reduce_fusion.6
  113.8 3.2 %collective-permute-done.5 = f32[256,128]{1,0:T(8,128)S(1)} collective-permute-done((f32[256,128]{1,0:T(8,128)S(1)}, f32[256,128]{1,0:T(8,128)S(1)}, u32[]{:S(2)}, u32[]{:S(2)}) %collective-permute-start.5) | collective-permute-done | bytes 131104 | tf_op jit(solution)/shard_map/ppermute | solution.py:20
  117.0 2.3 collective-permute-done.4
  119.4 10.8 %gather_fusion.2 = f32[4096,128]{1,0:T(8,128)S(1)} fusion(f32[768,128]{1,0:T(8,128)S(1)} %pad_maximum_fusion.2, s32[4096]{0:T(1024)S(1)} %fusion.4), kind=kCustom, calls=%fused_computation.2.clone | custom fusion | bytes 4210688 | tf_op jit(solution)/shard_map/jit(_take)/gather | solution.py:31
  130.1 2.1 broadcast_select_fusion.5
  132.3 0.7 add_reduce_fusion.5
  133.6 3.2 %collective-permute-done.7 = f32[256,128]{1,0:T(8,128)S(1)} collective-permute-done((f32[256,128]{1,0:T(8,128)S(1)}, f32[256,128]{1,0:T(8,128)S(1)}, u32[]{:S(2)}, u32[]{:S(2)}) %collective-permute-start.7) | collective-permute-done | bytes 131104 | tf_op jit(solution)/shard_map/ppermute | solution.py:20
  136.8 2.0 collective-permute-done.6
  138.9 10.8 %gather_fusion.3 = f32[4096,128]{1,0:T(8,128)S(1)} fusion(f32[768,128]{1,0:T(8,128)S(1)} %pad_maximum_fusion.3, s32[4096]{0:T(1024)S(1)} %fusion.4), kind=kCustom, calls=%fused_computation.3.clone | custom fusion | bytes 4210688 | tf_op jit(solution)/shard_map/jit(_take)/gather | solution.py:31
  149.6 2.1 broadcast_select_fusion.4
  151.8 0.7 add_reduce_fusion.4
  152.5 0.8 collective-permute-start.9
  153.4 2.9 %collective-permute-done.9 = f32[256,128]{1,0:T(8,128)S(1)} collective-permute-done((f32[256,128]{1,0:T(8,128)S(1)}, f32[256,128]{1,0:T(8,128)S(1)}, u32[]{:S(2)}, u32[]{:S(2)}) %collective-permute-start.9) | collective-permute-done | bytes 131104 | tf_op jit(solution)/shard_map/ppermute | solution.py:20
  156.3 2.3 collective-permute-done.8
  158.7 10.8 %gather_fusion.4 = f32[4096,128]{1,0:T(8,128)S(1)} fusion(f32[768,128]{1,0:T(8,128)S(1)} %pad_maximum_fusion.4, s32[4096]{0:T(1024)S(1)} %fusion.4), kind=kCustom, calls=%fused_computation.4.clone | custom fusion | bytes 4210688 | tf_op jit(solution)/shard_map/jit(_take)/gather | solution.py:31
  169.5 2.1 broadcast_select_fusion.3
  171.6 0.7 add_reduce_fusion.3
  172.9 3.2 %collective-permute-done.11 = f32[256,128]{1,0:T(8,128)S(1)} collective-permute-done((f32[256,128]{1,0:T(8,128)S(1)}, f32[256,128]{1,0:T(8,128)S(1)}, u32[]{:S(2)}, u32[]{:S(2)}) %collective-permute-start.11) | collective-permute-done | bytes 131104 | tf_op jit(solution)/shard_map/ppermute | solution.py:20
  176.1 2.0 collective-permute-done.10
  178.2 10.8 %gather_fusion.5 = f32[4096,128]{1,0:T(8,128)S(1)} fusion(f32[768,128]{1,0:T(8,128)S(1)} %pad_maximum_fusion.5, s32[4096]{0:T(1024)S(1)} %fusion.4), kind=kCustom, calls=%fused_computation.5.clone | custom fusion | bytes 4210688 | tf_op jit(solution)/shard_map/jit(_take)/gather | solution.py:31
  189.0 2.1 broadcast_select_fusion.2
  191.1 0.7 add_reduce_fusion.2
  191.8 0.8 collective-permute-start.13
  192.7 2.9 %collective-permute-done.13 = f32[256,128]{1,0:T(8,128)S(1)} collective-permute-done((f32[256,128]{1,0:T(8,128)S(1)}, f32[256,128]{1,0:T(8,128)S(1)}, u32[]{:S(2)}, u32[]{:S(2)}) %collective-permute-start.13) | collective-permute-done | bytes 131104 | tf_op jit(solution)/shard_map/ppermute | solution.py:20
  195.6 2.3 collective-permute-done.12
  198.0 10.8 %gather_fusion.6 = f32[4096,128]{1,0:T(8,128)S(1)} fusion(f32[768,128]{1,0:T(8,128)S(1)} %pad_maximum_fusion.6, s32[4096]{0:T(1024)S(1)} %fusion.4), kind=kCustom, calls=%fused_computation.6.clone | custom fusion | bytes 4210688 | tf_op jit(solution)/shard_map/jit(_take)/gather | solution.py:31
  208.8 2.1 broadcast_select_fusion.1
  210.9 0.7 add_reduce_fusion.1
  212.2 3.2 %collective-permute-done.15 = f32[256,128]{1,0:T(8,128)S(1)} collective-permute-done((f32[256,128]{1,0:T(8,128)S(1)}, f32[256,128]{1,0:T(8,128)S(1)}, u32[]{:S(2)}, u32[]{:S(2)}) %collective-permute-start.15) | collective-permute-done | bytes 131104 | tf_op jit(solution)/shard_map/ppermute | solution.py:20
  215.4 2.0 collective-permute-done.14
  217.5 10.8 %gather_fusion.7 = f32[4096,128]{1,0:T(8,128)S(1)} fusion(f32[768,128]{1,0:T(8,128)S(1)} %pad_maximum_fusion.7, s32[4096]{0:T(1024)S(1)} %fusion.4), kind=kCustom, calls=%fused_computation.7.clone | custom fusion | bytes 4210688 | tf_op jit(solution)/shard_map/jit(_take)/gather | solution.py:31
  228.3 2.1 broadcast_select_fusion
  231.5 0.8 copy.15
  (62 shorter events, 7.1 us)
Async XLA Ops:
  7.2 6.0 %copy-start = (f32[16]{0:T(128)S(1)}, f32[16]{0:T(128)}, u32[]{:S(2)}) copy-start(f32[16]{0:T(128)} %param.17) | copy-start | bytes 196
  7.2 53.2 %reduce-scatter.2.cloned.1.call-start = ((), (), s32[]{:S(2)}) async-start(), calls=%async_computation.1 | async-start | bytes 147456 | tf_op jit(solution)/shard_map/reduce_scatter | solution.py:56
  9.0 17.0 %collective-permute-start.1 = (f32[256,128]{1,0:T(8,128)S(1)}, f32[256,128]{1,0:T(8,128)S(1)}, u32[]{:S(2)}, u32[]{:S(2)}) collective-permute-start(f32[256,128]{1,0:T(8,128)S(1)} %bitcast_select_fusion), channel_id=1, source_target_pairs={{1,0},{2,1},{3,2},{4,3},{5,4},{6,5},{7,6},{0,7},{9,8},{10,9},{11,1... | collective-permute-start | bytes 393224 | tf_op jit(solution)/shard_map/ppermute | solution.py:20
  12.4 13.6 %collective-permute-start = (f32[256,128]{1,0:T(8,128)S(1)}, f32[256,128]{1,0:T(8,128)S(1)}, u32[]{:S(2)}, u32[]{:S(2)}) collective-permute-start(f32[256,128]{1,0:T(8,128)S(1)} %bitcast_select_fusion), channel_id=1, source_target_pairs={{0,1},{1,2},{2,3},{3,4},{4,5},{5,6},{6,7},{7,0},{8,9},{9,10},{10,1... | collective-permute-start | bytes 393224 | tf_op jit(solution)/shard_map/ppermute | solution.py:18
  26.1 47.8 %copy-start.5 = (f32[16,256]{1,0:T(8,128)S(1)}, f32[16,256]{1,0:T(8,128)}, u32[]{:S(2)}) copy-start(f32[16,256]{1,0:T(8,128)} %param.15) | copy-start | bytes 49156
  74.5 16.8 %copy-start.6 = (f32[16,256]{1,0:T(8,128)S(1)}, f32[16,256]{1,0:T(8,128)}, u32[]{:S(2)}) copy-start(f32[16,256]{1,0:T(8,128)} %param.14) | copy-start | bytes 49156
  74.5 16.8 %copy-start.7 = (f32[16,256]{1,0:T(8,128)S(1)}, f32[16,256]{1,0:T(8,128)}, u32[]{:S(2)}) copy-start(f32[16,256]{1,0:T(8,128)} %param.13) | copy-start | bytes 49156
  78.1 14.5 %copy-start.8 = (s32[128]{0:T(128)S(1)}, s32[128]{0:T(128)}, u32[]{:S(2)}) copy-start(s32[128]{0:T(128)} %param.11) | copy-start | bytes 1540
  92.6 17.7 %copy-start.3 = (f32[256,128]{1,0:T(8,128)}, f32[256,128]{1,0:T(8,128)S(1)}, u32[]{:S(2)}) copy-start(f32[256,128]{1,0:T(8,128)S(1)} %add_reduce_fusion.7) | copy-start | bytes 393220
  92.7 3.0 %collective-permute-start.3 = (f32[256,128]{1,0:T(8,128)S(1)}, f32[256,128]{1,0:T(8,128)S(1)}, u32[]{:S(2)}, u32[]{:S(2)}) collective-permute-start(f32[256,128]{1,0:T(8,128)S(1)} %fusion.5), channel_id=1, source_target_pairs={{1,0},{2,1},{3,2},{4,3},{5,4},{6,5},{7,6},{0,7},{9,8},{10,9},{11,1... | collective-permute-start | bytes 393224 | tf_op jit(solution)/shard_map/ppermute | solution.py:20
  92.8 6.7 %collective-permute-start.2 = (f32[256,128]{1,0:T(8,128)S(1)}, f32[256,128]{1,0:T(8,128)S(1)}, u32[]{:S(2)}, u32[]{:S(2)}) collective-permute-start(f32[256,128]{1,0:T(8,128)S(1)} %fusion.5), channel_id=1, source_target_pairs={{0,1},{1,2},{2,3},{3,4},{4,5},{5,6},{6,7},{7,0},{8,9},{9,10},{10,1... | collective-permute-start | bytes 393224 | tf_op jit(solution)/shard_map/ppermute | solution.py:18
  113.2 3.8 %collective-permute-start.5 = (f32[256,128]{1,0:T(8,128)S(1)}, f32[256,128]{1,0:T(8,128)S(1)}, u32[]{:S(2)}, u32[]{:S(2)}) collective-permute-start(f32[256,128]{1,0:T(8,128)S(1)} %min.49), channel_id=1, source_target_pairs={{1,0},{2,1},{3,2},{4,3},{5,4},{6,5},{7,6},{0,7},{9,8},{10,9},{11,1... | collective-permute-start | bytes 393224 | tf_op jit(solution)/shard_map/ppermute | solution.py:20
  113.3 6.0 %collective-permute-start.4 = (f32[256,128]{1,0:T(8,128)S(1)}, f32[256,128]{1,0:T(8,128)S(1)}, u32[]{:S(2)}, u32[]{:S(2)}) collective-permute-start(f32[256,128]{1,0:T(8,128)S(1)} %min.49), channel_id=1, source_target_pairs={{0,1},{1,2},{2,3},{3,4},{4,5},{5,6},{6,7},{7,0},{8,9},{9,10},{10,1... | collective-permute-start | bytes 393224 | tf_op jit(solution)/shard_map/ppermute | solution.py:18
  133.0 3.8 %collective-permute-start.7 = (f32[256,128]{1,0:T(8,128)S(1)}, f32[256,128]{1,0:T(8,128)S(1)}, u32[]{:S(2)}, u32[]{:S(2)}) collective-permute-start(f32[256,128]{1,0:T(8,128)S(1)} %min.51), channel_id=1, source_target_pairs={{1,0},{2,1},{3,2},{4,3},{5,4},{6,5},{7,6},{0,7},{9,8},{10,9},{11,1... | collective-permute-start | bytes 393224 | tf_op jit(solution)/shard_map/ppermute | solution.py:20
  133.5 5.3 %collective-permute-start.6 = (f32[256,128]{1,0:T(8,128)S(1)}, f32[256,128]{1,0:T(8,128)S(1)}, u32[]{:S(2)}, u32[]{:S(2)}) collective-permute-start(f32[256,128]{1,0:T(8,128)S(1)} %min.51), channel_id=1, source_target_pairs={{0,1},{1,2},{2,3},{3,4},{4,5},{5,6},{6,7},{7,0},{8,9},{9,10},{10,1... | collective-permute-start | bytes 393224 | tf_op jit(solution)/shard_map/ppermute | solution.py:18
  152.5 3.8 %collective-permute-start.9 = (f32[256,128]{1,0:T(8,128)S(1)}, f32[256,128]{1,0:T(8,128)S(1)}, u32[]{:S(2)}, u32[]{:S(2)}) collective-permute-start(f32[256,128]{1,0:T(8,128)S(1)} %min.53), channel_id=1, source_target_pairs={{1,0},{2,1},{3,2},{4,3},{5,4},{6,5},{7,6},{0,7},{9,8},{10,9},{11,1... | collective-permute-start | bytes 393224 | tf_op jit(solution)/shard_map/ppermute | solution.py:20
  153.3 5.3 %collective-permute-start.8 = (f32[256,128]{1,0:T(8,128)S(1)}, f32[256,128]{1,0:T(8,128)S(1)}, u32[]{:S(2)}, u32[]{:S(2)}) collective-permute-start(f32[256,128]{1,0:T(8,128)S(1)} %min.53), channel_id=1, source_target_pairs={{0,1},{1,2},{2,3},{3,4},{4,5},{5,6},{6,7},{7,0},{8,9},{9,10},{10,1... | collective-permute-start | bytes 393224 | tf_op jit(solution)/shard_map/ppermute | solution.py:18
  172.3 3.8 %collective-permute-start.11 = (f32[256,128]{1,0:T(8,128)S(1)}, f32[256,128]{1,0:T(8,128)S(1)}, u32[]{:S(2)}, u32[]{:S(2)}) collective-permute-start(f32[256,128]{1,0:T(8,128)S(1)} %min.55), channel_id=1, source_target_pairs={{1,0},{2,1},{3,2},{4,3},{5,4},{6,5},{7,6},{0,7},{9,8},{10,9},{11,1... | collective-permute-start | bytes 393224 | tf_op jit(solution)/shard_map/ppermute | solution.py:20
  172.8 5.3 %collective-permute-start.10 = (f32[256,128]{1,0:T(8,128)S(1)}, f32[256,128]{1,0:T(8,128)S(1)}, u32[]{:S(2)}, u32[]{:S(2)}) collective-permute-start(f32[256,128]{1,0:T(8,128)S(1)} %min.55), channel_id=1, source_target_pairs={{0,1},{1,2},{2,3},{3,4},{4,5},{5,6},{6,7},{7,0},{8,9},{9,10},{10,1... | collective-permute-start | bytes 393224 | tf_op jit(solution)/shard_map/ppermute | solution.py:18
  191.8 6.2 %copy-start.1 = (f32[256,128]{1,0:T(8,128)}, f32[256,128]{1,0:T(8,128)S(1)}, u32[]{:S(2)}) copy-start(f32[256,128]{1,0:T(8,128)S(1)} %add_reduce_fusion.2) | copy-start | bytes 393220
  191.8 3.8 %collective-permute-start.13 = (f32[256,128]{1,0:T(8,128)S(1)}, f32[256,128]{1,0:T(8,128)S(1)}, u32[]{:S(2)}, u32[]{:S(2)}) collective-permute-start(f32[256,128]{1,0:T(8,128)S(1)} %min.57), channel_id=1, source_target_pairs={{1,0},{2,1},{3,2},{4,3},{5,4},{6,5},{7,6},{0,7},{9,8},{10,9},{11,1... | collective-permute-start | bytes 393224 | tf_op jit(solution)/shard_map/ppermute | solution.py:20
  192.7 5.3 %collective-permute-start.12 = (f32[256,128]{1,0:T(8,128)S(1)}, f32[256,128]{1,0:T(8,128)S(1)}, u32[]{:S(2)}, u32[]{:S(2)}) collective-permute-start(f32[256,128]{1,0:T(8,128)S(1)} %min.57), channel_id=1, source_target_pairs={{0,1},{1,2},{2,3},{3,4},{4,5},{5,6},{6,7},{7,0},{8,9},{9,10},{10,1... | collective-permute-start | bytes 393224 | tf_op jit(solution)/shard_map/ppermute | solution.py:18
  211.6 3.8 %collective-permute-start.15 = (f32[256,128]{1,0:T(8,128)S(1)}, f32[256,128]{1,0:T(8,128)S(1)}, u32[]{:S(2)}, u32[]{:S(2)}) collective-permute-start(f32[256,128]{1,0:T(8,128)S(1)} %min.59), channel_id=1, source_target_pairs={{1,0},{2,1},{3,2},{4,3},{5,4},{6,5},{7,6},{0,7},{9,8},{10,9},{11,1... | collective-permute-start | bytes 393224 | tf_op jit(solution)/shard_map/ppermute | solution.py:20
  212.2 5.3 %collective-permute-start.14 = (f32[256,128]{1,0:T(8,128)S(1)}, f32[256,128]{1,0:T(8,128)S(1)}, u32[]{:S(2)}, u32[]{:S(2)}) collective-permute-start(f32[256,128]{1,0:T(8,128)S(1)} %min.59), channel_id=1, source_target_pairs={{0,1},{1,2},{2,3},{3,4},{4,5},{5,6},{6,7},{7,0},{8,9},{9,10},{10,1... | collective-permute-start | bytes 393224 | tf_op jit(solution)/shard_map/ppermute | solution.py:18
  230.4 0.9 copy-start.2
  230.4 1.0 copy-start.4
Sparse Core Ops, SparseCore 0:
  25.3 35.0 reduce-scatter.1
